TPU v7x, 128 devices: a whole 4x4x4 slice. The times are simulated.
128 devices in a mesh: tok: 8 (over z, core), head: 16 (over x, y).
Axes of the slice: x: 4, y: 4, z: 4, core: 2. Of those that a mesh axis runs over, the one named last changes fastest.
Arguments:
- queries: bfloat16 [4096, 16384], P('tok', 'head'), may hold values from -9 to 9
- keys: bfloat16 [4096, 1024], P('tok'), may hold values from -6 to 6
- values: bfloat16 [4096, 1024], P('tok'), may hold values from -6 to 6
- grad_out: bfloat16 [4096, 16384], P('tok', 'head'), may hold values from -6 to 6
- doc_ids: int32 [4096], P('tok'), may hold values from 0 to 5, never falling along the last dimension, each value on 1 to 2048 neighbouring positions
Outputs:
- attn_out: bfloat16 [4096, 16384], P('tok', 'head')
- grad_queries: bfloat16 [4096, 16384], P('tok', 'head')
- grad_keys: bfloat16 [4096, 1024], P(('tok', 'head'))
- grad_values: bfloat16 [4096, 1024], P(('tok', 'head'))
All inputs are finite; a program needn't handle non-finite values.
Results may differ from a plain program's by a relative error of at most 0.04.
Values may be sent and summed in bfloat16 or wider, within the bound.
A program may use at most 64 MiB of HBM per device.

v0:
```python
import jax
import jax.numpy as jnp
from jax import lax
from jax.sharding import PartitionSpec as P

KVH = 8
HD = 128


def side_by_side(arrays, axis, dim, along):
    columns = [a.reshape(*a.shape[:along], -1) for a in arrays]
    both = jnp.concatenate(columns, axis=along)
    result, at, finished = (lax.all_gather(both, axis, axis=dim, tiled=True), 0, [])
    for a, column in zip(arrays, columns):
        piece = result[..., at : at + column.shape[along]]
        finished.append(piece.reshape(*piece.shape[:along], *a.shape[along:]))
        at += column.shape[along]
    return tuple(finished)


def partner_2(shard, axis, stride):
    return lax.ppermute(shard, axis, [(i, i ^ 1 << stride) for i in range(lax.axis_size(axis))])


def side_by_side_2(arrays, axis, split_dim, concat_dim, along):
    both = jnp.concatenate(arrays, axis=along)
    result, at, finished = (
        lax.all_to_all(both, axis, split_axis=split_dim, concat_axis=concat_dim, tiled=True),
        0,
        [],
    )
    for a in arrays:
        finished.append(lax.slice_in_dim(result, at, at + a.shape[along], axis=along))
        at += a.shape[along]
    return tuple(finished)


def in_one_piece(arrays, axis, dim, along):
    widths = [a.shape[along] for a in arrays]
    both = jnp.concatenate(arrays, axis=along)
    result = lax.psum_scatter(both, axis, scatter_dimension=dim, tiled=True)
    return tuple(jnp.split(result, [sum(widths[:k]) for k in range(1, len(widths))], axis=along))


def doc_starts(all_docs, row_docs):
    earlier = all_docs[None, :] < row_docs[:, None]
    return jnp.sum(earlier.astype(jnp.int32), axis=1)


def attend(query_rows, grad_rows, first_pos, key_all, value_all, all_docs, grad_keys, grad_values):
    half_rows = query_rows.shape[0]
    local_heads = query_rows.shape[1] // HD
    score_scale = HD ** (-0.5)
    row_docs = lax.dynamic_slice_in_dim(all_docs, first_pos, half_rows)
    starts = doc_starts(all_docs, row_docs)
    positions = first_pos + jnp.arange(half_rows, dtype=jnp.int32)
    query_heads = query_rows.reshape(half_rows, local_heads, HD)
    grad_heads = grad_rows.reshape(half_rows, local_heads, HD)
    first_block = jnp.min(starts) // half_rows
    end_block = (first_pos + half_rows - 1) // half_rows + 1

    def tiles(key_block):
        key_tile = lax.dynamic_slice_in_dim(key_all, key_block * half_rows, half_rows, 0)
        value_tile = lax.dynamic_slice_in_dim(value_all, key_block * half_rows, half_rows, 0)
        key_pos = key_block * half_rows + jnp.arange(half_rows, dtype=jnp.int32)
        scores = (
            jnp.einsum("qhd,kd->hqk", query_heads, key_tile, preferred_element_type=jnp.float32)
            * score_scale
        )
        allowed = (key_pos[None, :] >= starts[:, None]) & (key_pos[None, :] <= positions[:, None])
        return (scores, allowed[None], key_tile, value_tile)

    def forward_step(key_block, state):
        running_max, running_sum, accumulated = state
        scores, allowed, key_tile, value_tile = tiles(key_block)
        block_max = jnp.max(jnp.where(allowed, scores, -1e30), axis=2)
        new_max = jnp.maximum(running_max, block_max)
        weights = jnp.where(allowed, jnp.exp(scores - new_max[:, :, None]), 0.0)
        rescale = jnp.exp(running_max - new_max)
        running_sum = running_sum * rescale + jnp.sum(weights, axis=2)
        update = jnp.einsum(
            "hqk,kd->hqd",
            weights.astype(jnp.bfloat16),
            value_tile,
            preferred_element_type=jnp.float32,
        )
        accumulated = accumulated * rescale[:, :, None] + update
        return (new_max, running_sum, accumulated)

    start_state = (
        jnp.full((local_heads, half_rows), -1e30, jnp.float32),
        jnp.zeros((local_heads, half_rows), jnp.float32),
        jnp.zeros((local_heads, half_rows, HD), jnp.float32),
    )
    running_max, running_sum, accumulated = lax.fori_loop(
        first_block, end_block, forward_step, start_state
    )
    output_f = accumulated / running_sum[:, :, None]
    log_total = running_max + jnp.log(running_sum)
    row_delta = jnp.einsum("qhd,hqd->hq", grad_heads.astype(jnp.float32), output_f)

    def backward_step(key_block, state):
        grad_query, grad_keys, grad_values = state
        scores, allowed, key_tile, value_tile = tiles(key_block)
        probs = jnp.where(allowed, jnp.exp(scores - log_total[:, :, None]), 0.0)
        probs_low = probs.astype(jnp.bfloat16)
        grad_probs = jnp.einsum(
            "qhd,kd->hqk", grad_heads, value_tile, preferred_element_type=jnp.float32
        )
        grad_scores = (probs * (grad_probs - row_delta[:, :, None])).astype(jnp.bfloat16)
        grad_query = grad_query + jnp.einsum(
            "hqk,kd->hqd", grad_scores, key_tile, preferred_element_type=jnp.float32
        )
        key_part = (
            jnp.einsum("hqk,qhd->kd", grad_scores, query_heads, preferred_element_type=jnp.float32)
            * score_scale
        )
        value_part = jnp.einsum(
            "hqk,qhd->kd", probs_low, grad_heads, preferred_element_type=jnp.float32
        )
        row_start = key_block * half_rows
        old_keys = lax.dynamic_slice_in_dim(grad_keys, row_start, half_rows, 0)
        old_values = lax.dynamic_slice_in_dim(grad_values, row_start, half_rows, 0)
        grad_keys = lax.dynamic_update_slice_in_dim(grad_keys, old_keys + key_part, row_start, 0)
        grad_values = lax.dynamic_update_slice_in_dim(
            grad_values, old_values + value_part, row_start, 0
        )
        return (grad_query, grad_keys, grad_values)

    back_state = (jnp.zeros((local_heads, half_rows, HD), jnp.float32), grad_keys, grad_values)
    grad_query, grad_keys, grad_values = lax.fori_loop(
        first_block, end_block, backward_step, back_state
    )
    output_rows = (
        output_f.transpose(1, 0, 2).reshape(half_rows, local_heads * HD).astype(jnp.bfloat16)
    )
    grad_query_rows = (
        (grad_query * score_scale)
        .transpose(1, 0, 2)
        .reshape(half_rows, local_heads * HD)
        .astype(jnp.bfloat16)
    )
    return (output_rows, grad_query_rows, grad_keys, grad_values)


def body(queries, keys, values, grad_out, doc_ids):
    tok_count = lax.axis_size("tok")
    head_count = lax.axis_size("head")
    tok_number = lax.axis_index("tok")
    head_number = lax.axis_index("head")
    dev_rows = queries.shape[0]
    half_rows = dev_rows // 2
    copy_count = head_count // KVH
    kv_group = head_number // copy_count
    key_own = lax.dynamic_slice_in_dim(keys, kv_group * HD, HD, 1)
    value_own = lax.dynamic_slice_in_dim(values, kv_group * HD, HD, 1)
    key_all, value_all, docs_low = side_by_side(
        (key_own, value_own, doc_ids.astype(jnp.bfloat16)), "tok", 0, 1
    )
    all_docs = docs_low.astype(jnp.int32)
    total_rows = key_all.shape[0]
    top_bit = tok_count.bit_length() - 2
    query_first, query_second = (queries[:half_rows], queries[half_rows:])
    grad_first, grad_second = (grad_out[:half_rows], grad_out[half_rows:])
    grad_keys = jnp.zeros((total_rows, HD), jnp.float32)
    grad_values = jnp.zeros((total_rows, HD), jnp.float32)
    upper = tok_number >= tok_count // 2
    partner = tok_number ^ tok_count // 2
    offset = jnp.where(upper, 0, half_rows).astype(jnp.int32)
    keep_query = jnp.where(upper, query_first, query_second)
    keep_grad = jnp.where(upper, grad_first, grad_second)
    moving = jnp.stack(
        [jnp.where(upper, query_second, query_first), jnp.where(upper, grad_second, grad_first)]
    )
    moving = partner_2(moving, "tok", top_bit)
    output_keep, grad_q_keep, grad_keys, grad_values = attend(
        keep_query,
        keep_grad,
        tok_number * dev_rows + offset,
        key_all,
        value_all,
        all_docs,
        grad_keys,
        grad_values,
    )
    output_moved, grad_q_moved, grad_keys, grad_values = attend(
        moving[0],
        moving[1],
        partner * dev_rows + offset,
        key_all,
        value_all,
        all_docs,
        grad_keys,
        grad_values,
    )
    coming = partner_2(jnp.stack([output_moved, grad_q_moved]), "tok", top_bit)
    output_first = jnp.where(upper, output_keep, coming[0])
    output_second = jnp.where(upper, coming[0], output_keep)
    grad_q_first = jnp.where(upper, grad_q_keep, coming[1])
    grad_q_second = jnp.where(upper, coming[1], grad_q_keep)
    attn_out = jnp.concatenate([output_first, output_second], axis=0)
    grad_queries = jnp.concatenate([grad_q_first, grad_q_second], axis=0)
    piece_rows = total_rows // (tok_count * head_count)
    shaped_keys = grad_keys.reshape(tok_count, head_count, piece_rows, HD)
    shaped_values = grad_values.reshape(tok_count, head_count, piece_rows, HD)
    mixed_keys, mixed_values = tuple(
        (
            part.astype(jnp.float32)
            for part in side_by_side_2(
                (shaped_keys.astype(jnp.bfloat16), shaped_values.astype(jnp.bfloat16)),
                "head",
                1,
                1,
                0,
            )
        )
    )
    paired_keys = mixed_keys.reshape(tok_count, KVH, copy_count, piece_rows, HD).sum(axis=2)
    paired_values = mixed_values.reshape(tok_count, KVH, copy_count, piece_rows, HD).sum(axis=2)
    summed_keys, summed_values = tuple(
        (
            part.astype(jnp.float32)
            for part in in_one_piece(
                (paired_keys.astype(jnp.bfloat16), paired_values.astype(jnp.bfloat16)), "tok", 0, 1
            )
        )
    )
    final_keys = summed_keys[0].transpose(1, 0, 2).reshape(piece_rows, KVH * HD)
    final_values = summed_values[0].transpose(1, 0, 2).reshape(piece_rows, KVH * HD)
    return (
        attn_out,
        grad_queries,
        final_keys.astype(jnp.bfloat16),
        final_values.astype(jnp.bfloat16),
    )


def solution(mesh):
    return jax.shard_map(
        body,
        mesh=mesh,
        in_specs=(P("tok", "head"), P("tok", None), P("tok", None), P("tok", "head"), P("tok")),
        out_specs=(
            P("tok", "head"),
            P("tok", "head"),
            P(("tok", "head"), None),
            P(("tok", "head"), None),
        ),
        check_vma=False,
    )
```

profile of v0, /device:TPU:1, one launch (start us, length us, event | category | flops | bytes accessed | tf_op | source)
XLA Modules:
  0.0 313.6 jit_solution(13223083587685583067)
XLA Ops:
  12.5 4.4 %collective-permute-start = (bf16[2,256,1024]{2,1,0:T(8,128)(2,1)}, bf16[2,256,1024]{2,1,0:T(8,128)(2,1)}, u32[]{:S(2)}, u32[]{:S(2)}) collective-permute-start(bf16[2,256,1024]{2,1,0:T(8,128)(2,1)} %pad_maximum_fusion.1), channel_id=1, source_target_pairs={{0,64},{16,80},{32,96},{48,112},{64,0},{80,16},{96,32},{112,48},{1... | collective-permute-start | bytes 3145736 | tf_op jit(solution)/shard_map/ppermute | solution.py:22
  18.3 34.1 %collective-permute-done = bf16[2,256,1024]{2,1,0:T(8,128)(2,1)} collective-permute-done((bf16[2,256,1024]{2,1,0:T(8,128)(2,1)}, bf16[2,256,1024]{2,1,0:T(8,128)(2,1)}, u32[]{:S(2)}, u32[]{:S(2)}) %collective-permute-start) | collective-permute-done | bytes 1048608 | tf_op jit(solution)/shard_map/ppermute | solution.py:22
  66.0 3.0 fusion.89
  69.1 7.8 %while.61 = (s32[]{:T(128)}, f32[8,256]{1,0:T(8,128)S(1)}, f32[8,256]{1,0:T(8,128)S(1)}, f32[8,256,128]{2,1,0:T(8,128)S(1)}, s32[]{:T(128)}, /*index=5*/s32[256]...) while((s32[]{:T(128)}, f32[8,256]{1,0:T(8,128)S(1)}, ...), condition=%wide.region_11.12_spmd.clone, body=%wide.region_8.11_spmd.clone.sunk | while | flops 274928128 | bytes 9442499 | solution.py:95
  74.9 1.9 convolution_add_fusion.9
  78.0 15.5 %while.60 = (s32[]{:T(128)}, f32[8,256]{1,0:T(8,128)S(1)}, f32[8,256]{1,0:T(8,128)S(1)}, f32[8,256,128]{2,1,0:T(8,128)S(1)}, s32[]{:T(128)}, /*index=5*/s32[256]...) while((s32[]{:T(128)}, f32[8,256]{1,0:T(8,128)S(1)}, ...), condition=%wide.region_5.6_spmd.clone, body=%wide.region_2.5_spmd.clone.sunk | while | flops 274928128 | bytes 9442499 | solution.py:95
  79.9 1.9 convolution_add_fusion.8
  87.7 1.9 convolution_add_fusion.8
  91.6 1.9 convolution_add_fusion.8
  93.5 2.4 convert_bitcast_fusion.1
  99.9 38.4 %while.62 = (s32[]{:T(128)}, f32[8,256,128]{2,1,0:T(8,128)}, f32[4096,128]{1,0:T(8,128)}, f32[4096,128]{1,0:T(8,128)}, s32[]{:T(128)}, /*index=5*/s32[256]{0:T(2...) while((s32[]{:T(128)}, f32[8,256,128]{2,1,0:T(8,128)}, ...), condition=%wide.region_13.14_spmd.clone, body=%wide.region_12.13_spmd.clone.sunk | while | flops 675316224 | bytes 14505191 | solution.py:131
  102.8 2.0 fusion.165
  104.8 2.0 fusion.166
  106.8 2.7 convolution_add_fusion.10
  112.4 2.0 fusion.165
  114.4 2.0 fusion.166
  116.4 2.7 convolution_add_fusion.10
  122.0 2.0 fusion.165
  124.0 2.0 fusion.166
  125.9 2.7 convolution_add_fusion.10
  131.5 2.0 fusion.165
  133.5 2.0 fusion.166
  135.5 2.7 convolution_add_fusion.10
  138.3 2.4 convert_bitcast_fusion
  140.7 16.7 %while.63 = (s32[]{:T(128)}, f32[8,256,128]{2,1,0:T(8,128)S(1)}, f32[4096,128]{1,0:T(8,128)}, f32[4096,128]{1,0:T(8,128)}, s32[]{:T(128)}, /*index=5*/s32[256]{0...) while((s32[]{:T(128)}, f32[8,256,128]{2,1,0:T(8,128)S(1)}, ...), condition=%wide.region_15.16_spmd.clone, body=%wide.region_14.15_spmd.clone.sunk | while | flops 675316224 | bytes 14505191 | solution.py:131
  143.6 2.0 fusion.179
  145.6 2.0 fusion.180
  152.0 2.0 fusion.179
  154.0 2.0 fusion.180
  160.5 24.2 %all_to_all.5 = bf16[16,16,32,128]{3,2,0,1:T(8,128)(2,1)S(1)} all-to-all(bf16[16,16,32,128]{3,2,0,1:T(8,128)(2,1)S(1)} %copy.90), channel_id=1, replica_groups=mesh['tok'=8,'head'=16] {'head'}, dimensions={1} | all-to-all | bytes 4194304 | tf_op jit(solution)/shard_map/all_to_all | solution.py:28
  189.7 13.5 %collective-permute-done.1 = bf16[2,256,1024]{2,1,0:T(8,128)(2,1)S(1)} collective-permute-done((bf16[2,256,1024]{2,1,0:T(8,128)(2,1)S(1)}, bf16[2,256,1024]{2,1,0:T(8,128)(2,1)S(1)}, u32[]{:S(2)}, u32[]{:S(2)}) %collective-permute-start.1) | collective-permute-done | bytes 1048608 | tf_op jit(solution)/shard_map/ppermute | solution.py:22
  207.1 97.5 %reduce-scatter.2.cloned.1.call-done = bf16[1,16,32,128]{3,2,1,0:T(8,128)(2,1)} async-done(((bf16[8,16,32,128]{3,2,1,0:T(8,128)(2,1)}), bf16[1,16,32,128]{3,2,1,0:T(8,128)(2,1)}) %reduce-scatter.2.cloned.1.call-update) | async-done | bytes 131088 | tf_op jit(solution)/shard_map/reduce_scatter | solution.py:41
  (141 shorter events, 69.3 us)
Async XLA Ops:
  7.2 2.9 copy-start.5
  7.2 47.9 %all-gather.2.cloned.1.call-start = ((), (), s32[]{:S(2)}) async-start(), calls=%async_computation.2 | async-start | bytes 3538944 | tf_op jit(solution)/shard_map/all_gather | solution.py:13
  10.0 294.6 %reduce-scatter.2.cloned.1.call-start = ((), (), s32[]{:S(2)}) async-start(), calls=%async_computation.3 | async-start | bytes 1179648 | tf_op jit(solution)/shard_map/reduce_scatter | solution.py:41
  12.5 39.9 %collective-permute-start = (bf16[2,256,1024]{2,1,0:T(8,128)(2,1)}, bf16[2,256,1024]{2,1,0:T(8,128)(2,1)}, u32[]{:S(2)}, u32[]{:S(2)}) collective-permute-start(bf16[2,256,1024]{2,1,0:T(8,128)(2,1)} %pad_maximum_fusion.1), channel_id=1, source_target_pairs={{0,64},{16,80},{32,96},{48,112},{64,0},{80,16},{96,32},{112,48},{1... | collective-permute-start | bytes 3145736 | tf_op jit(solution)/shard_map/ppermute | solution.py:22
  76.9 1.0 copy-start
  99.9 38.4 %copy-start.1 = (f32[8,256,128]{2,1,0:T(8,128)S(1)}, f32[8,256,128]{2,1,0:T(8,128)}, u32[]{:S(2)}) copy-start(f32[8,256,128]{2,1,0:T(8,128)} %copy-done) | copy-start | bytes 3145732
  157.5 2.2 copy-start.2
  186.3 1.0 copy-start.4
  187.3 15.9 %copy-start.3 = (bf16[8,32,8,128]{3,2,1,0:T(8,128)(2,1)S(1)}, bf16[8,32,8,128]{3,2,1,0:T(8,128)(2,1)}, u32[]{:S(2)}) copy-start(bf16[8,32,8,128]{3,2,1,0:T(8,128)(2,1)} %get-tuple-element.724) | copy-start | bytes 1572868
  188.0 15.2 %collective-permute-start.1 = (bf16[2,256,1024]{2,1,0:T(8,128)(2,1)S(1)}, bf16[2,256,1024]{2,1,0:T(8,128)(2,1)S(1)}, u32[]{:S(2)}, u32[]{:S(2)}) collective-permute-start(bf16[2,256,1024]{2,1,0:T(8,128)(2,1)S(1)} %pad_maximum_fusion.2), channel_id=1, source_target_pairs={{0,64},{16,80},{32,96},{48,112},{64,0},{80,16},{96,32},{112,48},{1... | collective-permute-start | bytes 3145736 | tf_op jit(solution)/shard_map/ppermute | solution.py:22
Sparse Core Ops, SparseCore 0:
  10.2 44.2 all-gather.1
  186.4 118.1 reduce-scatter.1
where the time goes:
time: 312 us; the launch traced here: 314 us
  waiting for transfers between devices  145 us (46%)
  matrix products  73.4 us (24%)
  other arithmetic  27.4 us (9%)
  blocking collectives  24.2 us (8%)
  between operations  19.6 us (6%)
  local copies, waits for them, and re-layouts  16.9 us (5%)
  starting transfers between devices  6.21 us (2%)
    reduce_scatter x1, waiting for transfers between devices, in_one_piece(): result = lax.psum_scatter(both, axis, scatter_dimension=dim, tiled=True)  97.5 us
    ppermute x2, waiting for transfers between devices, partner_2(): lax.ppermute(shard, axis, [(i, i ^ 1 << stride) for i in range(lax.axis_s...  47.6 us
    all_to_all x1, blocking collectives, side_by_side_2(): lax.all_to_all(both, axis, split_axis=split_dim, concat_axis=concat_dim,...  24.2 us
    dot_general x12, matrix products, tiles(): jnp.einsum('qhd,kd->hqk', query_heads, key_tile, preferred_element_type=j...  16.5 us
    dot_general x6, matrix products, backward_step(): jnp.einsum('hqk,kd->hqd', grad_scores, key_tile, preferred_element_type=j...  13.8 us
    dot_general x6, matrix products, backward_step(): jnp.einsum('hqk,qhd->kd', probs_low, grad_heads, preferred_element_type=j...  12 us
    dot_general x6, matrix products, backward_step(): jnp.einsum('hqk,qhd->kd', grad_scores, query_heads, preferred_element_typ...  12 us
    dot_general x6, matrix products, forward_step(): jnp.einsum('hqk,kd->hqd', weights.astype(jnp.bfloat16), value_tile, prefe...  11.4 us
  transfers between devices with their start and end apart: 4, of which 3 were waited for; matrix products, arithmetic and copies ran while one was open for 4% of the time, Pallas kernels for 0%

commit v1 on v0

v1 whole, which is shorter than its diff:
```python
import math

import jax
import jax.numpy as jnp
from jax import lax
from jax.experimental import pallas as pl
from jax.experimental.pallas import tpu as pltpu
from jax.sharding import PartitionSpec as P

KVH = 8
HD = 128
T = 256
REACH = 8
NT = REACH + 1
BIG = -131072.0
SCALE = HD**-0.5
EXP2_SCALE = SCALE * math.log2(math.e)
NEG = -1e30


def nt(a, b):
    return lax.dot_general(a, b, (((1,), (1,)), ((), ())), preferred_element_type=jnp.float32)


def nn(a, b):
    return lax.dot_general(a, b, (((1,), (0,)), ((), ())), preferred_element_type=jnp.float32)


def attend_kernel(
    q_ref, g_ref, k_ref, v_ref, e_ref, b_ref,
    out_ref, dq_ref, dkv_ref,
    kt_ref, vt_ref, s_ref, p_ref, ds_ref, dk_ref, dv_ref,
):
    tiles = k_ref.shape[0]
    heads = q_ref.shape[1] // HD

    def transpose_step(i, _):
        kt_ref[i] = k_ref[i].T
        vt_ref[i] = v_ref[i].T
        dk_ref[i] = jnp.zeros((T, HD), jnp.float32)
        dv_ref[i] = jnp.zeros((T, HD), jnp.float32)
        return 0

    lax.fori_loop(0, tiles, transpose_step, 0)

    key_pos = lax.broadcasted_iota(jnp.int32, (T, T), 0)
    row_pos = lax.broadcasted_iota(jnp.int32, (T, T), 1)

    def step(i, _):
        rb = i // heads
        h = i % heads
        rows = pl.ds(pl.multiple_of(rb * T, T), T)
        cols = pl.ds(pl.multiple_of(h * HD, HD), HD)
        q = q_ref[rows, cols]
        g = g_ref[rows, cols]
        q_ext = jnp.concatenate([q, b_ref[rows, :]], axis=1)
        gt = g.astype(jnp.float32).T
        top = jnp.full((8, T), NEG, jnp.float32)
        for j in range(NT):
            k_ext = jnp.concatenate([k_ref[rb + j], e_ref[rb + j]], axis=1)
            s = nt(k_ext, q_ext)
            if j == NT - 1:
                s = jnp.where(key_pos <= row_pos, s, BIG)
            s_ref[j] = s
            top = jnp.maximum(top, jnp.max(s.reshape(T // 8, 8, T), axis=0))
        top = jnp.max(top, axis=0, keepdims=True) * EXP2_SCALE
        total = jnp.zeros((8, T), jnp.float32)
        ot = jnp.zeros((HD, T), jnp.float32)
        for j in range(NT):
            p = jnp.exp2(s_ref[j] * EXP2_SCALE - top)
            total = total + jnp.sum(p.reshape(T // 8, 8, T), axis=0)
            pb = p.astype(jnp.bfloat16)
            p_ref[j] = pb
            ot = ot + nn(vt_ref[rb + j], pb)
        inverse = 1.0 / jnp.sum(total, axis=0, keepdims=True)
        ot = ot * inverse
        out_ref[rows, cols] = ot.T.astype(jnp.bfloat16)
        gn = (gt * inverse).astype(jnp.bfloat16)
        delta = jnp.sum(gn.astype(jnp.float32) * ot, axis=0, keepdims=True)
        dqt = jnp.zeros((HD, T), jnp.float32)
        for j in range(NT):
            dp = nn(v_ref[rb + j], gn)
            pb = p_ref[j]
            ds = (dp - delta).astype(jnp.bfloat16) * pb
            dqt = dqt + nn(kt_ref[rb + j], ds)
            dk_ref[rb + j] += nn(ds, q)
            dv_ref[rb + j] += nt(pb, gn)
        dq_ref[rows, cols] = (dqt * SCALE).T.astype(jnp.bfloat16)
        return 0

    lax.fori_loop(0, (q_ref.shape[0] // T) * heads, step, 0)

    def finish(i, _):
        dkv_ref[i, :, 0:HD] = (dk_ref[i] * SCALE).astype(jnp.bfloat16)
        dkv_ref[i, :, HD : 2 * HD] = dv_ref[i].astype(jnp.bfloat16)
        return 0

    lax.fori_loop(0, tiles, finish, 0)


def attend(q, g, k, v, e, b):
    tiles = k.shape[0]
    rows, width = q.shape
    pairs = (rows // T) * NT * T * T * (width // HD)
    return pl.pallas_call(
        attend_kernel,
        out_shape=(
            jax.ShapeDtypeStruct((rows, width), jnp.bfloat16),
            jax.ShapeDtypeStruct((rows, width), jnp.bfloat16),
            jax.ShapeDtypeStruct((tiles, T, 2 * HD), jnp.bfloat16),
        ),
        in_specs=[pl.BlockSpec(memory_space=pltpu.VMEM)] * 6,
        out_specs=[pl.BlockSpec(memory_space=pltpu.VMEM)] * 3,
        scratch_shapes=[
            pltpu.VMEM((tiles, HD, T), jnp.bfloat16),
            pltpu.VMEM((tiles, HD, T), jnp.bfloat16),
            pltpu.VMEM((NT, T, T), jnp.float32),
            pltpu.VMEM((NT, T, T), jnp.bfloat16),
            pltpu.VMEM((NT, T, T), jnp.bfloat16),
            pltpu.VMEM((tiles, T, HD), jnp.float32),
            pltpu.VMEM((tiles, T, HD), jnp.float32),
        ],
        compiler_params=pltpu.CompilerParams(vmem_limit_bytes=48 * 1024 * 1024),
        cost_estimate=pl.CostEstimate(
            flops=pairs * 12 * HD, bytes_accessed=rows * width * 8, transcendentals=pairs
        ),
    )(q, g, k, v, e, b)


def body(queries, keys, values, grad_out, doc_ids):
    tok_count = lax.axis_size("tok")
    head_count = lax.axis_size("head")
    tok_number = lax.axis_index("tok")
    head_number = lax.axis_index("head")
    rows = queries.shape[0]
    copies = head_count // KVH
    group = head_number // copies
    span = REACH * T
    key_own = lax.dynamic_slice_in_dim(keys, group * HD, HD, 1)
    value_own = lax.dynamic_slice_in_dim(values, group * HD, HD, 1)
    docs_own = doc_ids.astype(jnp.bfloat16)[:, None]
    packed = jnp.concatenate([key_own, value_own, docs_own], axis=1)
    gathered = lax.all_gather(packed, "tok", axis=0, tiled=True)
    padded = jnp.pad(gathered, ((span, 0), (0, 0)))
    local = lax.dynamic_slice_in_dim(padded, tok_number * rows, span + rows, 0)
    tiles = (span + rows) // T
    k = local[:, 0:HD].reshape(tiles, T, HD)
    v = local[:, HD : 2 * HD].reshape(tiles, T, HD)
    positions = tok_number * rows - span + jnp.arange(span + rows)
    docs = jnp.where(positions >= 0, local[:, 2 * HD].astype(jnp.int32), 6)
    lanes = jnp.arange(HD)[None, :]
    e = (docs[:, None] == lanes).astype(jnp.bfloat16).reshape(tiles, T, HD)
    b = jnp.where(doc_ids[:, None] == lanes, 0.0, BIG).astype(jnp.bfloat16)
    attn_out, grad_queries, dkv = attend(queries, grad_out, k, v, e, b)
    dkv = dkv.reshape(span + rows, 2 * HD)
    whole = jnp.zeros((span + tok_count * rows, 2 * HD), jnp.bfloat16)
    whole = lax.dynamic_update_slice_in_dim(whole, dkv, tok_number * rows, 0)[span:]
    mine = lax.psum_scatter(whole, "tok", scatter_dimension=0, tiled=True)
    piece = rows // head_count
    spread = lax.all_to_all(
        mine.reshape(head_count, piece, 2 * HD), "head", split_axis=0, concat_axis=0, tiled=True
    )
    final = spread.astype(jnp.float32).reshape(KVH, copies, piece, 2 * HD).sum(axis=1)
    final = final.astype(jnp.bfloat16).transpose(1, 0, 2)
    return (
        attn_out,
        grad_queries,
        final[:, :, :HD].reshape(piece, KVH * HD),
        final[:, :, HD:].reshape(piece, KVH * HD),
    )


def solution(mesh):
    return jax.shard_map(
        body,
        mesh=mesh,
        in_specs=(P("tok", "head"), P("tok", None), P("tok", None), P("tok", "head"), P("tok")),
        out_specs=(
            P("tok", "head"),
            P("tok", "head"),
            P(("tok", "head"), None),
            P(("tok", "head"), None),
        ),
        check_vma=False,
    )
```

time: 312 us -> 163 us (0.52)
  the two profiles are of different devices: /device:TPU:1 before, /device:TPU:0 now
where the time goes in v1:
time: 163 us
  waiting for transfers between devices  64.2 us (39%)
  Pallas kernels  58.8 us (36%)
  blocking collectives  15.2 us (9%)
  between operations  14.1 us (9%)
  local copies, waits for them, and re-layouts  5.77 us (4%)
  other arithmetic  4.51 us (3%)
    pallas_call x1, Pallas kernels, attend(): pl.pallas_call(attend_kernel, out_shape=(jax.ShapeDtypeStruct((rows, widt...  58.8 us
    reduce_scatter x1, waiting for transfers between devices, body(): mine = lax.psum_scatter(whole, 'tok', scatter_dimension=0, tiled=True)  34.3 us
    all_gather x1, waiting for transfers between devices, body(): gathered = lax.all_gather(packed, 'tok', axis=0, tiled=True)  29.9 us
    all_to_all x1, blocking collectives, body(): lax.all_to_all(mine.reshape(head_count, piece, 2 * HD), 'head', split_axi...  15.2 us
  transfers between devices with their start and end apart: 2, of which 2 were waited for; matrix products, arithmetic and copies ran while one was open for 1% of the time, Pallas kernels for 0%

profile of v1, /device:TPU:0, one launch (start us, length us, event | category | flops | bytes accessed | tf_op | source)
XLA Modules:
  0.0 162.7 jit_solution(14527851621561619796)
XLA Ops:
  7.2 0.0 all-gather.2.cloned.1.call-start
  7.2 0.7 convert_element_type.24
  7.9 0.1 broadcast_in_dim.26
  8.1 1.0 constant_dynamic-slice_fusion
  9.1 0.8 pad_maximum_fusion
  9.9 0.0 all-gather.2.cloned.1.call-update
  9.9 0.0 reduce-scatter.2.cloned.1.call-start
  9.9 0.8 select_convert_fusion.b_ref
  10.8 29.9 %all-gather.2.cloned.1.call-done = bf16[4096,257]{1,0:T(8,128)(2,1)} async-done(((bf16[512,257]{1,0:T(8,128)(2,1)}), bf16[4096,257]{1,0:T(8,128)(2,1)}) %all-gather.2.cloned.1.call-update) | async-done | bytes 2105360 | tf_op jit(solution)/shard_map/all_gather | solution.py:143
  40.7 0.0 copy-start.2
  40.7 1.7 %select_reduce_fusion = s32[2560]{0:T(1024)S(1)} fusion(s32[]{:T(128)S(6)} %select_n.24, s32[]{:T(128)S(6)} %add.33, bf16[4096,257]{1,0:T(8,128)(2,1)} %all-gather.2.cloned.1.call-done, s32[]{:T(128)S(6)} %sub.8), kind=kLoop, calls=%fused_computation.4 | loop fusion | flops 10240 | bytes 2115596 | tf_op jit(solution)/shard_map/jit(_where)/select_n | solution.py:150
  42.3 0.5 fusion.e_ref
  42.9 0.0 copy-done.2
  42.9 0.0 copy-start
  42.9 0.0 copy-start.1
  42.9 1.0 pad_dynamic-slice_fusion
  43.9 0.2 copy-done
  44.1 0.3 copy-done.1
  44.4 58.8 %shard_map.84 = (bf16[512,1024]{1,0:T(8,128)(2,1)}, bf16[512,1024]{1,0:T(8,128)(2,1)}, bf16[10,256,256]{2,1,0:T(8,128)(2,1)S(1)}) custom-call(bf16[512,1024]{1,0:T(8,128)(2,1)S(1)} %copy-done, bf16[512,1024]{1,0:T(8,128)(2,1)S(1)} %copy-done.1, bf16[10,256,128]{2,1,0:T(8,128)(2,1)S(1)} %bitcast.19, bf16[10,256,128]{2,1,0:T(8,128)(2,1)S(1)} %bitcast.18, ...), custom_call_target="tpu_custom_call" | custom-call | flops 14495514624 | bytes 4194304 | tf_op jit(solution)/shard_map/pallas_call | solution.py:105
  103.2 0.2 broadcast_in_dim.25
  103.4 0.1 constant_dynamic-update-slice_fusion
  103.5 1.5 slice.24
  105.0 0.0 reduce-scatter.2.cloned.1.call-update
  105.0 34.3 %reduce-scatter.2.cloned.1.call-done = bf16[512,256]{1,0:T(8,128)(2,1)} async-done(((bf16[4096,256]{1,0:T(8,128)(2,1)}), bf16[512,256]{1,0:T(8,128)(2,1)}) %reduce-scatter.2.cloned.1.call-update) | async-done | bytes 262160 | tf_op jit(solution)/shard_map/reduce_scatter | solution.py:158
  139.3 15.2 %all_to_all.5 = bf16[16,32,256]{2,1,0:T(8,128)(2,1)S(1)} all-to-all(bf16[16,32,256]{2,1,0:T(8,128)(2,1)} %bitcast.21), channel_id=1, replica_groups=mesh['tok'=8,'head'=16] {'head'}, dimensions={0} | all-to-all | bytes 524288 | tf_op jit(solution)/shard_map/all_to_all | solution.py:160
  154.5 0.6 copy.18
  155.2 0.6 copy.19
  (3 shorter events, 0.1 us)
Async XLA Ops:
  7.2 33.5 %all-gather.2.cloned.1.call-start = ((), (), s32[]{:S(2)}) async-start(), calls=%async_computation.2 | async-start | bytes 3538944 | tf_op jit(solution)/shard_map/all_gather | solution.py:143
  9.9 129.4 %reduce-scatter.2.cloned.1.call-start = ((), (), s32[]{:S(2)}) async-start(), calls=%async_computation.3 | async-start | bytes 2359296 | tf_op jit(solution)/shard_map/reduce_scatter | solution.py:158
  40.7 2.2 %copy-start.2 = (bf16[4096,257]{1,0:T(8,128)(2,1)S(1)}, bf16[4096,257]{1,0:T(8,128)(2,1)}, u32[]{:S(2)}) copy-start(bf16[4096,257]{1,0:T(8,128)(2,1)} %all-gather.2.cloned.1.call-done) | copy-start | bytes 6316036
  42.9 1.2 copy-start
  42.9 1.5 copy-start.1
Sparse Core Ops, SparseCore 0:
  10.2 30.3 all-gather.1
  105.1 34.0 reduce-scatter.1

commit v2 on v1

v2 whole, which is shorter than its diff:
```python
import math

import jax
import jax.numpy as jnp
from jax import lax
from jax.experimental import pallas as pl
from jax.experimental.pallas import tpu as pltpu
from jax.sharding import PartitionSpec as P

KVH = 8
HD = 128
T = 256
REACH = 8
NT = REACH + 1
BIG = -131072.0
SCALE = HD**-0.5
EXP2_SCALE = SCALE * math.log2(math.e)
NEG = -1e30


def nt(a, b):
    return lax.dot_general(a, b, (((1,), (1,)), ((), ())), preferred_element_type=jnp.float32)


def nn(a, b):
    return lax.dot_general(a, b, (((1,), (0,)), ((), ())), preferred_element_type=jnp.float32)


def attend_kernel(
    q_ref, g_ref, kv_ref, docs_ref,
    out_ref, dq_ref, dkv_ref,
    ke_ref, kt_ref, vt_ref, b_ref, s_ref, p_ref, ds_ref, dk_ref, dv_ref,
):
    tiles = ke_ref.shape[0]
    per_block = kv_ref.shape[1] // T
    heads = q_ref.shape[1] // HD
    half = T // HD
    kinds = lax.broadcasted_iota(jnp.int32, (HD, HD), 0)

    def prepare(i, _):
        block = i // per_block
        part = i % per_block
        rows = pl.ds(pl.multiple_of(part * T, T), T)
        key = kv_ref[block, rows, 0:HD]
        kt_ref[i] = key.T
        vt_ref[i] = kv_ref[block, rows, HD : 2 * HD].T
        ke_ref[i, :, 0:HD] = key
        for r in range(half):
            docs = docs_ref[block, pl.ds(part * half + r, 1), :]
            hot = jnp.where(docs == kinds, 1.0, 0.0)
            ke_ref[i, r * HD : (r + 1) * HD, HD : 2 * HD] = hot.T.astype(jnp.bfloat16)
        dk_ref[i] = jnp.zeros((T, HD), jnp.float32)
        dv_ref[i] = jnp.zeros((T, HD), jnp.float32)
        return 0

    lax.fori_loop(0, tiles, prepare, 0)
    last = kv_ref.shape[0] - 1
    for r in range(b_ref.shape[0] // HD):
        docs = docs_ref[last, r : r + 1, :]
        cold = jnp.where(docs == kinds, 0.0, BIG)
        b_ref[r * HD : (r + 1) * HD, :] = cold.T.astype(jnp.bfloat16)

    key_pos = lax.broadcasted_iota(jnp.int32, (T, T), 0)
    row_pos = lax.broadcasted_iota(jnp.int32, (T, T), 1)

    def step(i, _):
        rb = i // heads
        h = i % heads
        rows = pl.ds(pl.multiple_of(rb * T, T), T)
        cols = pl.ds(pl.multiple_of(h * HD, HD), HD)
        q = q_ref[rows, cols]
        g = g_ref[rows, cols]
        q_ext = jnp.concatenate([q, b_ref[rows, :]], axis=1)
        gt = g.astype(jnp.float32).T
        top = jnp.full((8, T), NEG, jnp.float32)
        for j in range(NT):
            s = nt(ke_ref[rb + j], q_ext)
            if j == NT - 1:
                s = jnp.where(key_pos <= row_pos, s, BIG)
            s_ref[j] = s
            top = jnp.maximum(top, jnp.max(s.reshape(T // 8, 8, T), axis=0))
        top = jnp.max(top, axis=0, keepdims=True) * EXP2_SCALE
        total = jnp.zeros((8, T), jnp.float32)
        ot = jnp.zeros((HD, T), jnp.float32)
        for j in range(NT):
            p = jnp.exp2(s_ref[j] * EXP2_SCALE - top)
            total = total + jnp.sum(p.reshape(T // 8, 8, T), axis=0)
            pb = p.astype(jnp.bfloat16)
            p_ref[j] = pb
            ot = ot + nn(vt_ref[rb + j], pb)
        inverse = 1.0 / jnp.sum(total, axis=0, keepdims=True)
        ot = ot * inverse
        out_ref[rows, cols] = ot.T.astype(jnp.bfloat16)
        gn = (gt * inverse).astype(jnp.bfloat16)
        delta = jnp.sum(gn.astype(jnp.float32) * ot, axis=0, keepdims=True)
        dqt = jnp.zeros((HD, T), jnp.float32)
        for j in range(NT):
            block = (rb + j) // per_block
            part = (rb + j) % per_block
            v = kv_ref[block, pl.ds(pl.multiple_of(part * T, T), T), HD : 2 * HD]
            dp = nn(v, gn)
            pb = p_ref[j]
            ds = (dp - delta).astype(jnp.bfloat16) * pb
            dqt = dqt + nn(kt_ref[rb + j], ds)
            dk_ref[rb + j] += nn(ds, q)
            dv_ref[rb + j] += nt(pb, gn)
        dq_ref[rows, cols] = (dqt * SCALE).T.astype(jnp.bfloat16)
        return 0

    lax.fori_loop(0, (q_ref.shape[0] // T) * heads, step, 0)

    def finish(i, _):
        rows = pl.ds(pl.multiple_of((i % per_block) * T, T), T)
        dkv_ref[i // per_block, rows, 0:HD] = (dk_ref[i] * SCALE).astype(jnp.bfloat16)
        dkv_ref[i // per_block, rows, HD : 2 * HD] = dv_ref[i].astype(jnp.bfloat16)
        return 0

    lax.fori_loop(0, tiles, finish, 0)


def attend(q, g, kv, docs):
    blocks, rows, _ = kv.shape
    tiles = blocks * rows // T
    width = q.shape[1]
    pairs = (rows // T) * NT * T * T * (width // HD)
    return pl.pallas_call(
        attend_kernel,
        out_shape=(
            jax.ShapeDtypeStruct((rows, width), jnp.bfloat16),
            jax.ShapeDtypeStruct((rows, width), jnp.bfloat16),
            jax.ShapeDtypeStruct((blocks, rows, 2 * HD), jnp.bfloat16),
        ),
        in_specs=[pl.BlockSpec(memory_space=pltpu.VMEM)] * 4,
        out_specs=[pl.BlockSpec(memory_space=pltpu.VMEM)] * 3,
        scratch_shapes=[
            pltpu.VMEM((tiles, T, 2 * HD), jnp.bfloat16),
            pltpu.VMEM((tiles, HD, T), jnp.bfloat16),
            pltpu.VMEM((tiles, HD, T), jnp.bfloat16),
            pltpu.VMEM((rows, HD), jnp.bfloat16),
            pltpu.VMEM((NT, T, T), jnp.float32),
            pltpu.VMEM((NT, T, T), jnp.bfloat16),
            pltpu.VMEM((NT, T, T), jnp.bfloat16),
            pltpu.VMEM((tiles, T, HD), jnp.float32),
            pltpu.VMEM((tiles, T, HD), jnp.float32),
        ],
        compiler_params=pltpu.CompilerParams(vmem_limit_bytes=48 * 1024 * 1024),
        cost_estimate=pl.CostEstimate(
            flops=pairs * 12 * HD, bytes_accessed=rows * width * 8, transcendentals=pairs
        ),
        name="attend",
    )(q, g, kv, docs)


def greet(peers):
    barrier = pltpu.get_barrier_semaphore()
    for peer in peers:
        pl.semaphore_signal(
            barrier, inc=1, device_id=peer, device_id_type=pl.DeviceIdType.MESH
        )
    pl.semaphore_wait(barrier, len(peers))


def others(axis):
    count = lax.axis_size(axis)
    me = lax.axis_index(axis)
    return [{axis: lax.rem(me + d, count)} for d in range(1, count)]


def gather_kernel(
    keys_ref, values_ref, docs_ref, kv_ref, all_docs_ref, load_sems, send_sems, recv_sems
):
    tok = lax.axis_index("tok")
    toks = lax.axis_size("tok")
    group = lax.axis_index("head") // (lax.axis_size("head") // KVH)
    blocks = kv_ref.shape[0]
    last = blocks - 1
    cols = pl.ds(pl.multiple_of(group * HD, HD), HD)
    loads = [
        pltpu.make_async_copy(keys_ref.at[:, cols], kv_ref.at[last, :, 0:HD], load_sems.at[0]),
        pltpu.make_async_copy(
            values_ref.at[:, cols], kv_ref.at[last, :, HD : 2 * HD], load_sems.at[1]
        ),
    ]
    for load in loads:
        load.start()
    all_docs_ref[last] = docs_ref[...]
    greet(others("tok"))
    for load in loads:
        load.wait()

    def copies(d, peer):
        return [
            pltpu.make_async_remote_copy(
                src_ref=kv_ref.at[last],
                dst_ref=kv_ref.at[last - d],
                send_sem=send_sems.at[0, d - 1],
                recv_sem=recv_sems.at[0, d - 1],
                device_id={"tok": peer},
                device_id_type=pl.DeviceIdType.MESH,
            ),
            pltpu.make_async_remote_copy(
                src_ref=docs_ref,
                dst_ref=all_docs_ref.at[last - d],
                send_sem=send_sems.at[1, d - 1],
                recv_sem=recv_sems.at[1, d - 1],
                device_id={"tok": peer},
                device_id_type=pl.DeviceIdType.MESH,
            ),
        ]

    for d in range(1, blocks):

        @pl.when(tok + d < toks)
        def _():
            for copy in copies(d, tok + d):
                copy.start()

        @pl.when(tok < d)
        def _():
            kv_ref[last - d] = jnp.zeros(kv_ref.shape[1:], jnp.bfloat16)
            all_docs_ref[last - d] = jnp.full(docs_ref.shape, 6, jnp.int32)

    for d in range(1, blocks):

        @pl.when(tok + d < toks)
        def _():
            for copy in copies(d, tok + d):
                copy.wait_send()

        @pl.when(tok >= d)
        def _():
            for copy in copies(d, tok - d):
                copy.wait_recv()


def gather(keys, values, docs, blocks):
    rows = keys.shape[0]
    vmem = pl.BlockSpec(memory_space=pltpu.VMEM)
    hbm = pl.BlockSpec(memory_space=pl.ANY)
    return pl.pallas_call(
        gather_kernel,
        out_shape=(
            jax.ShapeDtypeStruct((blocks, rows, 2 * HD), jnp.bfloat16),
            jax.ShapeDtypeStruct((blocks,) + docs.shape, jnp.int32),
        ),
        in_specs=[hbm, hbm, vmem],
        out_specs=[vmem, vmem],
        scratch_shapes=[
            pltpu.SemaphoreType.DMA((2,)),
            pltpu.SemaphoreType.DMA((2, blocks - 1)),
            pltpu.SemaphoreType.DMA((2, blocks - 1)),
        ],
        compiler_params=pltpu.CompilerParams(collective_id=0, has_side_effects=True),
        name="gather",
    )(keys, values, docs)


def reduce_kernel(
    dkv_ref, dk_ref, dv_ref, terms_ref, mid_ref, parts_ref, send_sems, recv_sems, out_sems, in_sems
):
    tok = lax.axis_index("tok")
    toks = lax.axis_size("tok")
    head = lax.axis_index("head")
    head_count = lax.axis_size("head")
    blocks = dkv_ref.shape[0]
    last = blocks - 1
    piece = mid_ref.shape[1]
    greet(others("tok") + others("head"))

    def term(d, peer):
        return pltpu.make_async_remote_copy(
            src_ref=dkv_ref.at[last - d],
            dst_ref=terms_ref.at[d - 1],
            send_sem=send_sems.at[d - 1],
            recv_sem=recv_sems.at[d - 1],
            device_id={"tok": peer},
            device_id_type=pl.DeviceIdType.MESH,
        )

    for d in range(1, blocks):

        @pl.when(tok >= d)
        def _():
            term(d, tok - d).start()

        @pl.when(tok + d >= toks)
        def _():
            terms_ref[d - 1] = jnp.zeros(terms_ref.shape[1:], jnp.bfloat16)

    for d in range(1, blocks):

        @pl.when(tok + d < toks)
        def _():
            term(d, tok + d).wait_recv()

    def add(i, _):
        rows = pl.ds(pl.multiple_of(i * piece, piece), piece)
        total = dkv_ref[last, rows, :].astype(jnp.float32)
        for d in range(1, blocks):
            total = total + terms_ref[d - 1, rows, :].astype(jnp.float32)
        mid_ref[i] = total.astype(jnp.bfloat16)
        return 0

    lax.fori_loop(0, head_count, add, 0)

    def part(d, peer, slot):
        return pltpu.make_async_remote_copy(
            src_ref=mid_ref.at[peer],
            dst_ref=parts_ref.at[slot],
            send_sem=out_sems.at[d - 1],
            recv_sem=in_sems.at[d - 1],
            device_id={"head": peer},
            device_id_type=pl.DeviceIdType.MESH,
        )

    for d in range(1, head_count):
        part(d, lax.rem(head + d, head_count), head).start()
    parts_ref[head] = mid_ref[head]
    for d in range(1, head_count):
        source = lax.rem(head + head_count - d, head_count)
        part(d, source, source).wait_recv()
    copies = head_count // KVH
    for g in range(KVH):
        total = parts_ref[g * copies].astype(jnp.float32)
        for c in range(1, copies):
            total = total + parts_ref[g * copies + c].astype(jnp.float32)
        total = total.astype(jnp.bfloat16)
        dk_ref[:, g * HD : (g + 1) * HD] = total[:, 0:HD]
        dv_ref[:, g * HD : (g + 1) * HD] = total[:, HD : 2 * HD]
    for d in range(1, blocks):

        @pl.when(tok >= d)
        def _():
            term(d, tok - d).wait_send()

    for d in range(1, head_count):
        part(d, lax.rem(head + d, head_count), head).wait_send()


def reduce(dkv, head_count):
    blocks, rows, width = dkv.shape
    piece = rows // head_count
    vmem = pl.BlockSpec(memory_space=pltpu.VMEM)
    return pl.pallas_call(
        reduce_kernel,
        out_shape=(jax.ShapeDtypeStruct((piece, KVH * HD), jnp.bfloat16),) * 2,
        in_specs=[vmem],
        out_specs=[vmem, vmem],
        scratch_shapes=[
            pltpu.VMEM((blocks - 1, rows, width), jnp.bfloat16),
            pltpu.VMEM((head_count, piece, width), jnp.bfloat16),
            pltpu.VMEM((head_count, piece, width), jnp.bfloat16),
            pltpu.SemaphoreType.DMA((blocks - 1,)),
            pltpu.SemaphoreType.DMA((blocks - 1,)),
            pltpu.SemaphoreType.DMA((head_count - 1,)),
            pltpu.SemaphoreType.DMA((head_count - 1,)),
        ],
        compiler_params=pltpu.CompilerParams(collective_id=1, has_side_effects=True),
        name="reduce",
    )(dkv)


def body(queries, keys, values, grad_out, doc_ids):
    rows = queries.shape[0]
    blocks = REACH * T // rows + 1
    docs = doc_ids.reshape(rows // HD, HD)
    kv, all_docs = gather(keys, values, docs, blocks)
    attn_out, grad_queries, dkv = attend(queries, grad_out, kv, all_docs)
    grad_keys, grad_values = reduce(dkv, lax.axis_size("head"))
    return attn_out, grad_queries, grad_keys, grad_values


def solution(mesh):
    return jax.shard_map(
        body,
        mesh=mesh,
        in_specs=(P("tok", "head"), P("tok", None), P("tok", None), P("tok", "head"), P("tok")),
        out_specs=(
            P("tok", "head"),
            P("tok", "head"),
            P(("tok", "head"), None),
            P(("tok", "head"), None),
        ),
        check_vma=False,
    )
```

time: 163 us -> 127 us (0.78)
  the two profiles are of different devices: /device:TPU:0 before, /device:TPU:32 now
where the time goes in v2:
time: 127 us
  Pallas kernels  120 us (94%)
  local copies, waits for them, and re-layouts  6.04 us (5%)
    pallas_call x1, Pallas kernels, attend(): pl.pallas_call(attend_kernel, out_shape=(jax.ShapeDtypeStruct((rows, widt...  59.4 us
    pallas_call x1, Pallas kernels, reduce(): pl.pallas_call(reduce_kernel, out_shape=(jax.ShapeDtypeStruct((piece, KVH...  43.8 us
    pallas_call x1, Pallas kernels, gather(): pl.pallas_call(gather_kernel, out_shape=(jax.ShapeDtypeStruct((blocks, ro...  16.9 us
    unnamed x12, local copies, waits for them, and re-layouts  6.04 us

profile of v2, /device:TPU:32, one launch (start us, length us, event | category | flops | bytes accessed | tf_op | source)
XLA Modules:
  0.0 126.9 jit_solution(4404906440417527972)
XLA Ops:
  0.6 0.0 copy-start.3
  0.6 0.0 copy-start.2
  0.7 16.9 %gather.1 = (bf16[5,512,256]{2,1,0:T(8,128)(2,1)}, s32[5,4,128]{2,1,0:T(4,128)}) custom-call(bf16[512,1024]{1,0:T(8,128)(2,1)} %keys_ref.1, bf16[512,1024]{1,0:T(8,128)(2,1)} %values_ref.1, s32[4,128]{1,0:T(4,128)} %bitcast.1), custom_call_target="tpu_custom_call" | custom-call | tf_op jit(solution)/shard_map/gather/pallas_call | solution.py:240
  17.6 0.0 copy-done.3
  17.6 0.0 copy-done.2
  17.6 0.0 copy-start.1
  17.6 1.3 %copy-done.1 = bf16[5,512,256]{2,1,0:T(8,128)(2,1)S(1)} copy-done((bf16[5,512,256]{2,1,0:T(8,128)(2,1)S(1)}, bf16[5,512,256]{2,1,0:T(8,128)(2,1)}, u32[]{:S(2)}) %copy-start.1) | copy-done | bytes 1310744
  18.9 0.0 copy-start.4
  18.9 0.7 copy-done.4
  19.6 59.4 %attend.1 = (bf16[512,1024]{1,0:T(8,128)(2,1)}, bf16[512,1024]{1,0:T(8,128)(2,1)}, bf16[5,512,256]{2,1,0:T(8,128)(2,1)S(1)}) custom-call(bf16[512,1024]{1,0:T(8,128)(2,1)S(1)} %copy-done.2, bf16[512,1024]{1,0:T(8,128)(2,1)S(1)} %copy-done.3, bf16[5,512,256]{2,1,0:T(8,128)(2,1)S(1)} %copy-done.1, s32[5,4,128]{2,1,0:T(4,128)S(1)} %copy-done.4), custom_call_target="tpu_custom_call" | custom-call | flops 14495514624 | bytes 4194304 | tf_op jit(solution)/shard_map/attend/pallas_call | solution.py:126
  79.0 0.0 copy-start
  79.0 1.1 copy-done
  80.1 43.8 %reduce.1 = (bf16[32,1024]{1,0:T(8,128)(2,1)}, bf16[32,1024]{1,0:T(8,128)(2,1)}) custom-call(bf16[5,512,256]{2,1,0:T(8,128)(2,1)} %copy-done), custom_call_target="tpu_custom_call" | custom-call | tf_op jit(solution)/shard_map/reduce/pallas_call | solution.py:344
  123.9 1.5 %copy.11 = bf16[32,1024]{1,0:T(8,128)(2,1)} copy(bf16[32,1024]{1,0:T(8,128)(2,1)} %get-tuple-element.24) | data formatting | bytes 131072
  125.4 1.5 %copy.12 = bf16[32,1024]{1,0:T(8,128)(2,1)} copy(bf16[32,1024]{1,0:T(8,128)(2,1)} %get-tuple-element.25) | data formatting | bytes 131072
Async XLA Ops:
  0.6 17.0 %copy-start.3 = (bf16[512,1024]{1,0:T(8,128)(2,1)S(1)}, bf16[512,1024]{1,0:T(8,128)(2,1)}, u32[]{:S(2)}) copy-start(bf16[512,1024]{1,0:T(8,128)(2,1)} %g_ref.1) | copy-start | bytes 3145732
  0.6 17.0 %copy-start.2 = (bf16[512,1024]{1,0:T(8,128)(2,1)S(1)}, bf16[512,1024]{1,0:T(8,128)(2,1)}, u32[]{:S(2)}) copy-start(bf16[512,1024]{1,0:T(8,128)(2,1)} %q_ref.1) | copy-start | bytes 3145732
  17.6 1.3 %copy-start.1 = (bf16[5,512,256]{2,1,0:T(8,128)(2,1)S(1)}, bf16[5,512,256]{2,1,0:T(8,128)(2,1)}, u32[]{:S(2)}) copy-start(bf16[5,512,256]{2,1,0:T(8,128)(2,1)} %get-tuple-element.11.kv_ref) | copy-start | bytes 3932164
  18.9 0.7 copy-start.4
  79.0 1.1 copy-start

commit v3 on v2

--- a/solution.py
+++ b/solution.py
@@ -12,6 +12,7 @@
 T = 256
 REACH = 8
 NT = REACH + 1
+GROUPS = [(j, min(2, NT - j)) for j in range(0, NT, 2)]
 BIG = -131072.0
 SCALE = HD**-0.5
 EXP2_SCALE = SCALE * math.log2(math.e)
@@ -29,11 +30,13 @@
 def attend_kernel(
     q_ref, g_ref, kv_ref, docs_ref,
     out_ref, dq_ref, dkv_ref,
-    ke_ref, kt_ref, vt_ref, b_ref, s_ref, p_ref, ds_ref, dk_ref, dv_ref,
+    ke_ref, kt_ref, v_ref, vt_ref, bt_ref, s_ref, p_ref, dk_ref, dv_ref,
+    top_ref, total_ref, ot_ref, dqt_ref,
 ):
     tiles = ke_ref.shape[0]
     per_block = kv_ref.shape[1] // T
     heads = q_ref.shape[1] // HD
+    units = (q_ref.shape[0] // T) * heads
     half = T // HD
     kinds = lax.broadcasted_iota(jnp.int32, (HD, HD), 0)
 
@@ -42,8 +45,10 @@
         part = i % per_block
         rows = pl.ds(pl.multiple_of(part * T, T), T)
         key = kv_ref[block, rows, 0:HD]
+        value = kv_ref[block, rows, HD : 2 * HD]
         kt_ref[i] = key.T
-        vt_ref[i] = kv_ref[block, rows, HD : 2 * HD].T
+        vt_ref[i] = value.T
+        v_ref[i] = value
         ke_ref[i, :, 0:HD] = key
         for r in range(half):
             docs = docs_ref[block, pl.ds(part * half + r, 1), :]
@@ -54,60 +59,106 @@
         return 0
 
     lax.fori_loop(0, tiles, prepare, 0)
+    dqt_ref[...] = jnp.zeros(dqt_ref.shape, jnp.float32)
     last = kv_ref.shape[0] - 1
-    for r in range(b_ref.shape[0] // HD):
+    for r in range(per_block * half):
         docs = docs_ref[last, r : r + 1, :]
-        cold = jnp.where(docs == kinds, 0.0, BIG)
-        b_ref[r * HD : (r + 1) * HD, :] = cold.T.astype(jnp.bfloat16)
+        cold = jnp.where(docs == kinds, 0.0, BIG).astype(jnp.bfloat16)
+        bt_ref[r // half, :, (r % half) * HD : (r % half + 1) * HD] = cold
 
     key_pos = lax.broadcasted_iota(jnp.int32, (T, T), 0)
     row_pos = lax.broadcasted_iota(jnp.int32, (T, T), 1)
 
-    def step(i, _):
+    def place(i):
         rb = i // heads
         h = i % heads
-        rows = pl.ds(pl.multiple_of(rb * T, T), T)
-        cols = pl.ds(pl.multiple_of(h * HD, HD), HD)
-        q = q_ref[rows, cols]
-        g = g_ref[rows, cols]
-        q_ext = jnp.concatenate([q, b_ref[rows, :]], axis=1)
-        gt = g.astype(jnp.float32).T
-        top = jnp.full((8, T), NEG, jnp.float32)
-        for j in range(NT):
-            s = nt(ke_ref[rb + j], q_ext)
-            if j == NT - 1:
-                s = jnp.where(key_pos <= row_pos, s, BIG)
-            s_ref[j] = s
-            top = jnp.maximum(top, jnp.max(s.reshape(T // 8, 8, T), axis=0))
-        top = jnp.max(top, axis=0, keepdims=True) * EXP2_SCALE
-        total = jnp.zeros((8, T), jnp.float32)
-        ot = jnp.zeros((HD, T), jnp.float32)
-        for j in range(NT):
-            p = jnp.exp2(s_ref[j] * EXP2_SCALE - top)
-            total = total + jnp.sum(p.reshape(T // 8, 8, T), axis=0)
-            pb = p.astype(jnp.bfloat16)
-            p_ref[j] = pb
-            ot = ot + nn(vt_ref[rb + j], pb)
-        inverse = 1.0 / jnp.sum(total, axis=0, keepdims=True)
-        ot = ot * inverse
-        out_ref[rows, cols] = ot.T.astype(jnp.bfloat16)
-        gn = (gt * inverse).astype(jnp.bfloat16)
-        delta = jnp.sum(gn.astype(jnp.float32) * ot, axis=0, keepdims=True)
-        dqt = jnp.zeros((HD, T), jnp.float32)
-        for j in range(NT):
-            block = (rb + j) // per_block
-            part = (rb + j) % per_block
-            v = kv_ref[block, pl.ds(pl.multiple_of(part * T, T), T), HD : 2 * HD]
-            dp = nn(v, gn)
-            pb = p_ref[j]
-            ds = (dp - delta).astype(jnp.bfloat16) * pb
-            dqt = dqt + nn(kt_ref[rb + j], ds)
-            dk_ref[rb + j] += nn(ds, q)
-            dv_ref[rb + j] += nt(pb, gn)
-        dq_ref[rows, cols] = (dqt * SCALE).T.astype(jnp.bfloat16)
+        return rb, pl.ds(pl.multiple_of(rb * T, T), T), pl.ds(pl.multiple_of(h * HD, HD), HD)
+
+    def flush(i):
+        _, rows, cols = place(i)
+        dq_ref[rows, cols] = (dqt_ref[...] * SCALE).T.astype(jnp.bfloat16)
+
+    def stage(a, b, c, flush_before):
+        if flush_before is not None:
+            flush(flush_before)
+        if a is not None:
+            ra, rows, cols = place(a)
+            q = q_ref[rows, cols]
+            inverse = 1.0 / jnp.sum(total_ref[...], axis=0, keepdims=True)
+            ot = ot_ref[...] * inverse
+            out_ref[rows, cols] = ot.T.astype(jnp.bfloat16)
+            gn = (g_ref[rows, cols].T.astype(jnp.float32) * inverse).astype(jnp.bfloat16)
+            delta = jnp.sum(gn.astype(jnp.float32) * ot, axis=0, keepdims=True)
+            gr = gn.T
+            dqt = jnp.zeros((HD, T), jnp.float32)
+        if b is not None:
+            rb, _, _ = place(b)
+            top = jnp.max(top_ref[...], axis=0, keepdims=True) * EXP2_SCALE
+            total = jnp.zeros((8, T), jnp.float32)
+            acc = jnp.zeros((HD, T), jnp.float32)
+        if c is not None:
+            rc, rows_c, cols_c = place(c)
+            qt = jnp.concatenate([q_ref[rows_c, cols_c].T, bt_ref[rc]], axis=0)
+            peak = jnp.full((8, T), NEG, jnp.float32)
+        def scores():
+            return nn(ke_ref[pl.ds(rc + j, n)].reshape(n * T, 2 * HD), qt)
+
+        def slopes():
+            return nn(v_ref[pl.ds(ra + j, n)].reshape(n * T, HD), gn)
+
+        for j, n in GROUPS:
+            if a is not None:
+                pa = p_ref[j : j + n].reshape(n * T, T)
+                if j > 0:
+                    dp = slopes()
+            if b is not None:
+                old = s_ref[j : j + n].reshape(n * T, T)
+            if c is not None:
+                s = scores()
+            if a is not None and j > 0:
+                dv_ref[pl.ds(ra + j, n)] += nn(pa, gr).reshape(n, T, HD)
+            if b is not None:
+                p = jnp.exp2(old * EXP2_SCALE - top)
+                total = total + jnp.sum(p.reshape(n * T // 8, 8, T), axis=0)
+                pb = p.astype(jnp.bfloat16)
+                p_ref[j : j + n] = pb.reshape(n, T, T)
+                for m in range(n):
+                    acc = acc + nn(vt_ref[rb + j + m], pb[m * T : (m + 1) * T])
+            if a is not None and j == 0:
+                dp = slopes()
+                dv_ref[pl.ds(ra + j, n)] += nn(pa, gr).reshape(n, T, HD)
+            if c is not None:
+                s = s.reshape(n, T, T)
+                for m in range(n):
+                    piece = s[m]
+                    if j + m == NT - 1:
+                        piece = jnp.where(key_pos <= row_pos, piece, BIG)
+                    s_ref[j + m] = piece
+                    peak = jnp.maximum(peak, jnp.max(piece.reshape(T // 8, 8, T), axis=0))
+            if a is not None:
+                ds = (dp - delta).astype(jnp.bfloat16) * pa
+                for m in range(n):
+                    dqt = dqt + nn(kt_ref[ra + j + m], ds[m * T : (m + 1) * T])
+                dk_ref[pl.ds(ra + j, n)] += nn(ds, q).reshape(n, T, HD)
+        if a is not None:
+            dqt_ref[...] = dqt
+        if b is not None:
+            total_ref[...] = total
+            ot_ref[...] = acc
+        if c is not None:
+            top_ref[...] = peak
+
+    stage(None, None, 0, None)
+    stage(None, 0, 1, None)
+
+    def main(i, _):
+        stage(i, i + 1, i + 2, jnp.maximum(i - 1, 0))
         return 0
 
-    lax.fori_loop(0, (q_ref.shape[0] // T) * heads, step, 0)
+    lax.fori_loop(0, units - 2, main, 0)
+    stage(units - 2, units - 1, None, units - 3)
+    stage(units - 1, None, None, units - 2)
+    flush(units - 1)
 
     def finish(i, _):
         rows = pl.ds(pl.multiple_of((i % per_block) * T, T), T)
@@ -135,13 +186,17 @@
         scratch_shapes=[
             pltpu.VMEM((tiles, T, 2 * HD), jnp.bfloat16),
             pltpu.VMEM((tiles, HD, T), jnp.bfloat16),
+            pltpu.VMEM((tiles, T, HD), jnp.bfloat16),
             pltpu.VMEM((tiles, HD, T), jnp.bfloat16),
-            pltpu.VMEM((rows, HD), jnp.bfloat16),
+            pltpu.VMEM((rows // T, HD, T), jnp.bfloat16),
             pltpu.VMEM((NT, T, T), jnp.float32),
-            pltpu.VMEM((NT, T, T), jnp.bfloat16),
             pltpu.VMEM((NT, T, T), jnp.bfloat16),
             pltpu.VMEM((tiles, T, HD), jnp.float32),
             pltpu.VMEM((tiles, T, HD), jnp.float32),
+            pltpu.VMEM((8, T), jnp.float32),
+            pltpu.VMEM((8, T), jnp.float32),
+            pltpu.VMEM((HD, T), jnp.float32),
+            pltpu.VMEM((HD, T), jnp.float32),
         ],
         compiler_params=pltpu.CompilerParams(vmem_limit_bytes=48 * 1024 * 1024),
         cost_estimate=pl.CostEstimate(

time: 127 us -> 103 us (0.81)
  Pallas kernels: 120 us -> 95.7 us
    pallas_call x1, Pallas kernels: 59.4 us -> 35 us  [attend(): pl.pallas_call(attend_kernel, out_shape=(jax.ShapeDtypeStruct((rows, widt...]
where the time goes in v3:
time: 103 us; the launch traced here: 102 us
  Pallas kernels  95.7 us (93%)
  local copies, waits for them, and re-layouts  6.04 us (6%)
    pallas_call x1, Pallas kernels, reduce(): pl.pallas_call(reduce_kernel, out_shape=(jax.ShapeDtypeStruct((piece, KVH...  43.8 us
    pallas_call x1, Pallas kernels, attend(): pl.pallas_call(attend_kernel, out_shape=(jax.ShapeDtypeStruct((rows, widt...  35 us
    pallas_call x1, Pallas kernels, gather(): pl.pallas_call(gather_kernel, out_shape=(jax.ShapeDtypeStruct((blocks, ro...  16.9 us
    unnamed x12, local copies, waits for them, and re-layouts  6.04 us

profile of v3, /device:TPU:32, one launch (start us, length us, event | category | flops | bytes accessed | tf_op | source)
XLA Modules:
  0.0 102.4 jit_solution(17783541041777465864)
XLA Ops:
  0.6 0.0 copy-start.3
  0.6 0.0 copy-start.2
  0.7 16.9 %gather.1 = (bf16[5,512,256]{2,1,0:T(8,128)(2,1)}, s32[5,4,128]{2,1,0:T(4,128)}) custom-call(bf16[512,1024]{1,0:T(8,128)(2,1)} %keys_ref.1, bf16[512,1024]{1,0:T(8,128)(2,1)} %values_ref.1, s32[4,128]{1,0:T(4,128)} %bitcast.1), custom_call_target="tpu_custom_call" | custom-call | tf_op jit(solution)/shard_map/gather/pallas_call | solution.py:295
  17.6 0.0 copy-done.3
  17.6 0.0 copy-done.2
  17.6 0.0 copy-start.1
  17.6 1.3 %copy-done.1 = bf16[5,512,256]{2,1,0:T(8,128)(2,1)S(1)} copy-done((bf16[5,512,256]{2,1,0:T(8,128)(2,1)S(1)}, bf16[5,512,256]{2,1,0:T(8,128)(2,1)}, u32[]{:S(2)}) %copy-start.1) | copy-done | bytes 1310744
  18.9 0.0 copy-start.4
  18.9 0.7 copy-done.4
  19.6 35.0 %attend.1 = (bf16[512,1024]{1,0:T(8,128)(2,1)}, bf16[512,1024]{1,0:T(8,128)(2,1)}, bf16[5,512,256]{2,1,0:T(8,128)(2,1)S(1)}) custom-call(bf16[512,1024]{1,0:T(8,128)(2,1)S(1)} %copy-done.2, bf16[512,1024]{1,0:T(8,128)(2,1)S(1)} %copy-done.3, bf16[5,512,256]{2,1,0:T(8,128)(2,1)S(1)} %copy-done.1, s32[5,4,128]{2,1,0:T(4,128)S(1)} %copy-done.4), custom_call_target="tpu_custom_call" | custom-call | flops 14495514624 | bytes 4194304 | tf_op jit(solution)/shard_map/attend/pallas_call | solution.py:177
  54.6 0.0 copy-start
  54.6 1.1 %copy-done = bf16[5,512,256]{2,1,0:T(8,128)(2,1)} copy-done((bf16[5,512,256]{2,1,0:T(8,128)(2,1)}, bf16[5,512,256]{2,1,0:T(8,128)(2,1)S(1)}, u32[]{:S(2)}) %copy-start) | copy-done | bytes 1310744
  55.7 43.8 %reduce.1 = (bf16[32,1024]{1,0:T(8,128)(2,1)}, bf16[32,1024]{1,0:T(8,128)(2,1)}) custom-call(bf16[5,512,256]{2,1,0:T(8,128)(2,1)} %copy-done), custom_call_target="tpu_custom_call" | custom-call | tf_op jit(solution)/shard_map/reduce/pallas_call | solution.py:399
  99.5 1.5 %copy.11 = bf16[32,1024]{1,0:T(8,128)(2,1)} copy(bf16[32,1024]{1,0:T(8,128)(2,1)} %get-tuple-element.24) | data formatting | bytes 131072
  101.0 1.5 %copy.12 = bf16[32,1024]{1,0:T(8,128)(2,1)} copy(bf16[32,1024]{1,0:T(8,128)(2,1)} %get-tuple-element.25) | data formatting | bytes 131072
Async XLA Ops:
  0.6 17.0 %copy-start.3 = (bf16[512,1024]{1,0:T(8,128)(2,1)S(1)}, bf16[512,1024]{1,0:T(8,128)(2,1)}, u32[]{:S(2)}) copy-start(bf16[512,1024]{1,0:T(8,128)(2,1)} %g_ref.1) | copy-start | bytes 3145732
  0.6 17.0 %copy-start.2 = (bf16[512,1024]{1,0:T(8,128)(2,1)S(1)}, bf16[512,1024]{1,0:T(8,128)(2,1)}, u32[]{:S(2)}) copy-start(bf16[512,1024]{1,0:T(8,128)(2,1)} %q_ref.1) | copy-start | bytes 3145732
  17.6 1.3 %copy-start.1 = (bf16[5,512,256]{2,1,0:T(8,128)(2,1)S(1)}, bf16[5,512,256]{2,1,0:T(8,128)(2,1)}, u32[]{:S(2)}) copy-start(bf16[5,512,256]{2,1,0:T(8,128)(2,1)} %get-tuple-element.11.kv_ref) | copy-start | bytes 3932164
  18.9 0.7 copy-start.4
  54.6 1.1 %copy-start = (bf16[5,512,256]{2,1,0:T(8,128)(2,1)}, bf16[5,512,256]{2,1,0:T(8,128)(2,1)S(1)}, u32[]{:S(2)}) copy-start(bf16[5,512,256]{2,1,0:T(8,128)(2,1)S(1)} %get-tuple-element.15.dkv_ref) | copy-start | bytes 3932164
